TPU v7x, 32 devices: a whole 2x2x4 slice. The times are simulated.
32 devices in a mesh: dp: 8 (over z, y), mp: 2 (over core), fsdp: 2 (over x).
Axes of the slice: x: 2, y: 2, z: 4, core: 2. Of those that a mesh axis runs over, the one named last changes fastest.
Arguments:
- features: bfloat16 [5, 1024, 512], P(None, ('dp', 'fsdp')), may hold values from -6 to 6
- memory_bank: bfloat16 [512, 32, 1024], P(('dp', 'fsdp')), may hold values from -1 to 1
- memory_fill: int32 [512], P(('dp', 'fsdp')), may hold values from 0 to 32
- left_keys: bfloat16 [512, 64, 1024], P(('dp', 'fsdp'), None, 'mp'), may hold values from -400 to 400
- left_values: bfloat16 [512, 64, 1024], P(('dp', 'fsdp'), None, 'mp'), may hold values from -6 to 6
- left_length: int32 [512], P(('dp', 'fsdp')), may hold values from 0 to 64
- w_query: bfloat16 [1024, 1024], P('fsdp', 'mp'), may hold values from -0.1875 to 0.1875
- w_key: bfloat16 [1024, 1024], P('fsdp', 'mp'), may hold values from -0.1875 to 0.1875
- w_value: bfloat16 [1024, 1024], P('fsdp', 'mp'), may hold values from -0.1875 to 0.1875
- w_out: bfloat16 [1024, 1024], P('mp', 'fsdp'), may hold values from -0.1875 to 0.1875
- w_up: bfloat16 [1024, 4096], P('fsdp', 'mp'), may hold values from -0.1875 to 0.1875
- w_down: bfloat16 [4096, 1024], P('mp', 'fsdp'), may hold values from -0.09375 to 0.09375
- out_gain: float32 [1024], replicated, may hold values from 0.1 to 1.9
Outputs:
- layer_out: bfloat16 [512, 5, 1024], P(('dp', 'fsdp'))
- memory_next: bfloat16 [512, 1024], P(('dp', 'fsdp'))
- center_keys: bfloat16 [512, 4, 1024], P(('dp', 'fsdp'), None, 'mp')
- center_values: bfloat16 [512, 4, 1024], P(('dp', 'fsdp'), None, 'mp')
All inputs are finite; a program needn't handle non-finite values.
Results may differ from a plain program's by a relative error of at most 0.0095.
Values may be sent and summed in bfloat16 or wider, within the bound.
A program may use at most 128 MiB of HBM per device.

v0:
```python
import jax
import jax.numpy as jnp
from jax import lax
from jax.sharding import PartitionSpec as P

HD = 64
GROUP = 4
epsilon = 1e-05
masked_score = -1e30


def normalize(values):
    values = values.astype(jnp.float32)
    average = jnp.mean(values, axis=-1, keepdims=True)
    centred = values - average
    variance = jnp.mean(centred * centred, axis=-1, keepdims=True)
    return centred * lax.rsqrt(variance + epsilon)


def matmul(left, right):
    return jnp.dot(left, right, preferred_element_type=jnp.float32)


def shards(
    features,
    memory_bank,
    memory_fill,
    left_keys,
    left_values,
    left_length,
    w_query,
    w_key,
    w_value,
    w_out,
    w_up,
    w_down,
    out_gain,
):
    frames, width_dev, all_streams = features.shape
    streams, mem_slots, width = memory_bank.shape
    left_slots = left_keys.shape[1]
    head_cols = w_query.shape[1]
    head_count = head_cols // HD
    flattened = features.reshape(frames * width_dev, all_streams)
    n_dp = lax.axis_size("dp")
    n_fsdp = lax.axis_size("fsdp")
    arrived = lax.all_to_all(flattened, ("dp", "fsdp"), split_axis=1, concat_axis=0, tiled=True)
    arrived = arrived.reshape(n_dp * n_fsdp, frames, width_dev, streams)
    inputs = jnp.transpose(arrived, (3, 1, 0, 2)).reshape(streams, frames, width)
    normed = normalize(inputs).astype(jnp.bfloat16)
    summary = jnp.mean(normed[:, :GROUP, :].astype(jnp.float32), axis=1).astype(jnp.bfloat16)
    query_rows = jnp.concatenate([normed, summary[:, None, :]], axis=1).reshape(-1, width)
    key_rows = jnp.concatenate([normed.reshape(-1, width), memory_bank.reshape(-1, width)], axis=0)
    query_sums = matmul(query_rows, lax.all_gather(w_query, "fsdp", axis=0, tiled=True))
    key_sums = matmul(key_rows, lax.all_gather(w_key, "fsdp", axis=0, tiled=True))
    value_sums = matmul(key_rows, lax.all_gather(w_value, "fsdp", axis=0, tiled=True))
    query_proj = query_sums.astype(jnp.bfloat16)
    key_proj = key_sums.astype(jnp.bfloat16)
    value_proj = value_sums.astype(jnp.bfloat16)
    group_total = streams * frames
    query_h = query_proj.reshape(streams, frames + 1, head_count, HD)
    ckey_h = key_proj[:group_total].reshape(streams, frames, head_count, HD)
    cval_h = value_proj[:group_total].reshape(streams, frames, head_count, HD)
    mkey_h = key_proj[group_total:].reshape(streams, mem_slots, head_count, HD)
    mval_h = value_proj[group_total:].reshape(streams, mem_slots, head_count, HD)
    lkey_h = left_keys.reshape(streams, left_slots, head_count, HD)
    lval_h = left_values.reshape(streams, left_slots, head_count, HD)
    not_summary = jnp.arange(frames + 1, dtype=jnp.int32) < frames
    mem_ok = jnp.arange(mem_slots, dtype=jnp.int32)[None, :] >= (mem_slots - memory_fill)[:, None]
    mem_mask = mem_ok[:, None, None, :] & not_summary[None, None, :, None]
    left_ok = (
        jnp.arange(left_slots, dtype=jnp.int32)[None, :] >= (left_slots - left_length)[:, None]
    )
    left_mask = left_ok[:, None, None, :]
    scale = HD ** (-0.5)
    score_mem = (
        jnp.einsum("sqhd,skhd->shqk", query_h, mkey_h, preferred_element_type=jnp.float32) * scale
    )
    score_left = (
        jnp.einsum("sqhd,skhd->shqk", query_h, lkey_h, preferred_element_type=jnp.float32) * scale
    )
    score_group = (
        jnp.einsum("sqhd,skhd->shqk", query_h, ckey_h, preferred_element_type=jnp.float32) * scale
    )
    score_mem = jnp.where(mem_mask, score_mem, masked_score)
    score_left = jnp.where(left_mask, score_left, masked_score)
    top = jnp.maximum(
        jnp.maximum(
            jnp.max(score_mem, axis=-1, keepdims=True), jnp.max(score_left, axis=-1, keepdims=True)
        ),
        jnp.max(score_group, axis=-1, keepdims=True),
    )
    exp_mem = jnp.exp(score_mem - top)
    exp_left = jnp.exp(score_left - top)
    exp_group = jnp.exp(score_group - top)
    totals = (
        jnp.sum(exp_mem, axis=-1, keepdims=True)
        + jnp.sum(exp_left, axis=-1, keepdims=True)
        + jnp.sum(exp_group, axis=-1, keepdims=True)
    )
    prob_mem = (exp_mem / totals).astype(jnp.bfloat16)
    prob_left = (exp_left / totals).astype(jnp.bfloat16)
    prob_group = (exp_group / totals).astype(jnp.bfloat16)
    attended = jnp.einsum("shqk,skhd->sqhd", prob_mem, mval_h, preferred_element_type=jnp.float32)
    attended = attended + jnp.einsum(
        "shqk,skhd->sqhd", prob_left, lval_h, preferred_element_type=jnp.float32
    )
    attended = attended + jnp.einsum(
        "shqk,skhd->sqhd", prob_group, cval_h, preferred_element_type=jnp.float32
    )
    attended = attended.astype(jnp.bfloat16).reshape(streams * (frames + 1), head_cols)
    attn_part = matmul(attended, lax.all_gather(w_out, "fsdp", axis=1, tiled=True))
    attn_out = (
        lax.psum(attn_part.astype(jnp.bfloat16), "mp")
        .astype(jnp.float32)
        .reshape(streams, frames + 1, width)
    )
    memory_next = jnp.tanh(attn_out[:, frames, :]).astype(jnp.bfloat16)
    hidden_state = inputs.astype(jnp.float32) + attn_out[:, :frames, :]
    h_norm = normalize(hidden_state).astype(jnp.bfloat16).reshape(-1, width)
    halves = lax.all_to_all(h_norm, "fsdp", split_axis=1, concat_axis=0, tiled=True)
    up_sums = lax.psum_scatter(
        matmul(halves, w_up).astype(jnp.bfloat16), "fsdp", scatter_dimension=0, tiled=True
    ).astype(jnp.float32)
    hidden = jax.nn.gelu(up_sums, approximate=True).astype(jnp.bfloat16)
    down_all = matmul(lax.all_gather(hidden, "fsdp", axis=0, tiled=True), w_down)
    down_part = lax.all_to_all(
        down_all.astype(jnp.bfloat16), "fsdp", split_axis=0, concat_axis=1, tiled=True
    ).astype(down_all.dtype)
    down_proj = lax.psum(down_part.astype(jnp.bfloat16), "mp").astype(jnp.float32)
    layer_out = (
        (normalize(hidden_state.reshape(-1, width) + down_proj) * out_gain)
        .astype(jnp.bfloat16)
        .reshape(streams, frames, width)
    )
    center_keys = key_proj[:group_total].reshape(streams, frames, head_cols)[:, :GROUP, :]
    center_values = value_proj[:group_total].reshape(streams, frames, head_cols)[:, :GROUP, :]
    return (layer_out, memory_next, center_keys, center_values)


def solution(mesh):
    in_specs = (
        P(None, ("dp", "fsdp"), None),
        P(("dp", "fsdp"), None, None),
        P(("dp", "fsdp")),
        P(("dp", "fsdp"), None, "mp"),
        P(("dp", "fsdp"), None, "mp"),
        P(("dp", "fsdp")),
        P("fsdp", "mp"),
        P("fsdp", "mp"),
        P("fsdp", "mp"),
        P("mp", "fsdp"),
        P("fsdp", "mp"),
        P("mp", "fsdp"),
        P(),
    )
    out_specs = (
        P(("dp", "fsdp"), None, None),
        P(("dp", "fsdp"), None),
        P(("dp", "fsdp"), None, "mp"),
        P(("dp", "fsdp"), None, "mp"),
    )
    return jax.shard_map(shards, mesh=mesh, in_specs=in_specs, out_specs=out_specs, check_vma=False)
```

profile of v0, /device:TPU:0, one launch (start us, length us, event | category | flops | bytes accessed | tf_op | source)
XLA Modules:
  0.0 236.4 jit_solution(17857175718315085044)
XLA Ops:
  12.6 8.3 %all-to-all-start = ((bf16[320,16,32]{0,2,1:T(8,128)(2,1)}), bf16[320,16,32]{0,2,1:T(8,128)(2,1)S(1)}, u32[]{:S(2)}, u32[]{:S(2)}) async-start(bf16[320,16,32]{0,2,1:T(8,128)(2,1)} %all_to_all.38), calls=%async_computation | async-start | bytes 786432 | tf_op jit(solution)/shard_map/all_to_all | solution.py:47
  21.6 6.2 %reshape.219 = bf16[32,64,8,64]{3,2,1,0:T(8,128)(2,1)} reshape(bf16[32,64,512]{2,1,0:T(8,128)(2,1)} %param.16) | data formatting | bytes 4194304 | tf_op jit(solution)/shard_map/reshape | solution.py:66
  27.8 6.2 %reshape.221 = bf16[32,64,8,64]{3,2,1,0:T(8,128)(2,1)} reshape(bf16[32,64,512]{2,1,0:T(8,128)(2,1)} %param.17) | data formatting | bytes 4194304 | tf_op jit(solution)/shard_map/reshape | solution.py:67
  40.1 3.6 %copy.121 = f32[32,5,16,64]{3,2,0,1:T(8,128)} copy(f32[32,5,16,64]{3,1,0,2:T(8,128)} %bitcast.51) | data formatting | bytes 1310720 | tf_op jit(solution)/shard_map/convert_element_type | solution.py:119
  51.6 3.4 %convolution_convert_fusion = bf16[1184,512]{1,0:T(8,128)(2,1)S(1)} fusion(bf16[1024,512]{1,0:T(8,128)(2,1)} %all-gather.10.cloned.1.call-done, bf16[1024,1024]{1,0:T(8,128)(2,1)} %bitcast.57, bf16[160,1024]{1,0:T(8,128)(2,1)} %multiply_convert_fusion.3), kind=kOutput, calls=%fused_computation.4 | convolution fusion | flops 1246969856 | bytes 4685824 | tf_op jit(solution)/shard_map/dot_general | solution.py:21
  56.7 3.9 %all-gather.8.cloned.1.call-done = bf16[1024,512]{1,0:T(8,128)(2,1)} async-done(((bf16[512,512]{1,0:T(8,128)(2,1)}), bf16[1024,512]{1,0:T(8,128)(2,1)}) %all-gather.8.cloned.1.call-update) | async-done | bytes 1048592 | tf_op jit(solution)/shard_map/all_gather | solution.py:54
  63.6 3.9 %reshape.218 = bf16[32,32,8,64]{3,2,1,0:T(8,128)(2,1)} reshape(bf16[1024,512]{1,0:T(8,128)(2,1)} %slice.40) | data formatting | bytes 2097152 | tf_op jit(solution)/shard_map/reshape | solution.py:64
  68.1 3.8 %fusion.63 = (f32[32,8,6]{2,1,0:T(8,128)S(1)}, f32[32,8,6,32]{3,2,1,0:T(8,128)S(1)}) fusion(bf16[32,32,8,64]{3,2,1,0:T(8,128)(2,1)} %reshape.218, bf16[32,6,8,64]{3,2,1,0:T(8,128)(2,1)S(1)} %reshape.217, pred[32,6,32]{2,1,0:T(8,128)(4,1)S(1)} %broadcast_and_fusion), kind=kOutput, calls=%fused_computation.93 | convolution fusion | flops 6437376 | bytes 1454080 | tf_op jit(solution)/shard_map/sqhd,skhd->shqk/dot_general | solution.py:77
  71.8 2.4 fusion.64
  77.0 6.5 %all-gather.6.cloned.1.call-done = bf16[1024,512]{1,0:T(8,128)(2,1)} async-done(((bf16[512,512]{1,0:T(8,128)(2,1)}), bf16[1024,512]{1,0:T(8,128)(2,1)}) %all-gather.6.cloned.1.call-update) | async-done | bytes 1048592 | tf_op jit(solution)/shard_map/all_gather | solution.py:56
  83.5 3.4 %convolution_convert_fusion.1 = bf16[1184,512]{1,0:T(8,128)(2,1)S(1)} fusion(bf16[1024,512]{1,0:T(8,128)(2,1)} %all-gather.6.cloned.1.call-done, bf16[1024,1024]{1,0:T(8,128)(2,1)} %bitcast.58, bf16[160,1024]{1,0:T(8,128)(2,1)} %multiply_convert_fusion.3), kind=kOutput, calls=%fused_computation.5 | convolution fusion | flops 1246969856 | bytes 4685824 | tf_op jit(solution)/shard_map/dot_general | solution.py:21
  88.9 3.0 %convolution_bitcast_fusion = f32[32,6,8,64]{3,1,2,0:T(8,128)} fusion(f32[32,8,6,5]{2,3,1,0:T(8,128)} %copy-done.6, bf16[32,5,8,64]{3,2,1,0:T(8,128)(2,1)} %reshape.222, f32[32,8,6]{2,1,0:T(8,128)S(1)} %add_add_fusion, f32[32,8,6]{2,1,0:T(8,128)S(1)} %maximum_maximum_fusion), kind=kOutput, calls=%fused_computation.23 | convolution fusion | flops 1006080 | bytes 600064 | tf_op jit(solution)/shard_map/shqk,skhd->sqhd/dot_general | solution.py:108
  93.0 3.9 %reshape.215 = bf16[32,32,8,64]{3,2,1,0:T(8,128)(2,1)} reshape(bf16[1024,512]{1,0:T(8,128)(2,1)} %slice.38) | data formatting | bytes 2097152 | tf_op jit(solution)/shard_map/reshape | solution.py:65
  96.9 2.7 %fusion.8 = f32[32,6,8,64]{3,1,2,0:T(8,128)S(1)} fusion(bf16[32,32,8,64]{3,2,1,0:T(8,128)(2,1)} %reshape.215, f32[32,8,6,32]{3,2,1,0:T(8,128)} %copy-done.7, f32[32,8,6]{2,1,0:T(8,128)S(1)} %copy-done.17, f32[32,8,6]{2,1,0:T(8,128)S(1)} %maximum_maximum_fusion), kind=kOutput, calls=%fused_computation.17 | convolution fusion | flops 6438912 | bytes 1650688 | tf_op jit(solution)/shard_map/shqk,skhd->sqhd/dot_general | solution.py:104
  102.4 3.8 %all-gather.12.cloned.1.call-done = bf16[512,1024]{1,0:T(8,128)(2,1)} async-done(((bf16[512,512]{1,0:T(8,128)(2,1)}), bf16[512,1024]{1,0:T(8,128)(2,1)}) %all-gather.12.cloned.1.call-update) | async-done | bytes 1048592 | tf_op jit(solution)/shard_map/all_gather | solution.py:112
  106.2 2.4 convolution_convert_fusion.3
  110.8 18.5 %all-reduce.3.cloned.1.call-done = bf16[32,6,1024]{2,0,1:T(8,128)(2,1)} async-done(((bf16[32,6,1024]{2,0,1:T(8,128)(2,1)}), bf16[32,6,1024]{2,0,1:T(8,128)(2,1)}) %all-reduce.3.cloned.1.call-update) | async-done | bytes 393232 | tf_op jit(solution)/shard_map/psum | solution.py:114
  133.8 9.1 %all_to_all.51 = bf16[160,2,512]{2,0,1:T(8,128)(2,1)S(1)} all-to-all(bf16[160,2,512]{2,0,1:T(8,128)(2,1)S(1)} %copy.143), channel_id=1, replica_groups=mesh['dp'=8,'mp'=2,'fsdp'=2] {'fsdp'}, dimensions={1} | all-to-all | bytes 655360 | tf_op jit(solution)/shard_map/all_to_all | solution.py:121
  145.2 23.3 %reduce-scatter.2.cloned.1.call-done = bf16[160,2048]{1,0:T(8,128)(2,1)} async-done(((bf16[320,2048]{1,0:T(8,128)(2,1)}), bf16[160,2048]{1,0:T(8,128)(2,1)}) %reduce-scatter.2.cloned.1.call-update) | async-done | bytes 655376 | tf_op jit(solution)/shard_map/reduce_scatter | solution.py:122
  168.5 2.4 %fusion.37 = bf16[160,2048]{1,0:T(8,128)(2,1)} fusion(bf16[160,2048]{1,0:T(8,128)(2,1)} %reduce-scatter.2.cloned.1.call-done), kind=kLoop, calls=%fused_computation.32 | loop fusion | flops 3276800 | bytes 1310720 | tf_op jit(solution)/shard_map/convert_element_type | solution.py:125
  171.0 24.3 %all-gather.14.cloned.1.call-done = bf16[320,2048]{1,0:T(8,128)(2,1)} async-done(((bf16[160,2048]{1,0:T(8,128)(2,1)}), bf16[320,2048]{1,0:T(8,128)(2,1)}) %all-gather.14.cloned.1.call-update) | async-done | bytes 1310736 | tf_op jit(solution)/shard_map/all_gather | solution.py:126
  195.3 2.8 %convolution_convert_fusion.4 = bf16[320,512]{1,0:T(8,128)(2,1)S(1)} fusion(bf16[320,2048]{1,0:T(8,128)(2,1)} %all-gather.14.cloned.1.call-done, bf16[2048,512]{1,0:T(8,128)(2,1)} %param.24), kind=kOutput, calls=%fused_computation.35 | convolution fusion | flops 671252480 | bytes 3735552 | tf_op jit(solution)/shard_map/dot_general | solution.py:21
  198.1 8.5 %all_to_all.52 = bf16[2,160,512]{2,1,0:T(8,128)(2,1)S(1)} all-to-all(bf16[2,160,512]{2,1,0:T(8,128)(2,1)S(1)} %bitcast.56), channel_id=1, replica_groups=mesh['dp'=8,'mp'=2,'fsdp'=2] {'fsdp'}, dimensions={0} | all-to-all | bytes 655360 | tf_op jit(solution)/shard_map/all_to_all | solution.py:127
  214.9 11.0 %all-reduce.5.cloned.1.call-done = bf16[160,1024]{1,0:T(8,128)(2,1)} async-done(((bf16[160,1024]{1,0:T(8,128)(2,1)}), bf16[160,1024]{1,0:T(8,128)(2,1)}) %all-reduce.5.cloned.1.call-update) | async-done | bytes 327696 | tf_op jit(solution)/shard_map/psum | solution.py:130
  (136 shorter events, 54.6 us)
Async XLA Ops:
  7.2 135.8 %copy-start = (bf16[512,2048]{1,0:T(8,128)(2,1)S(1)}, bf16[512,2048]{1,0:T(8,128)(2,1)}, u32[]{:S(2)}) copy-start(bf16[512,2048]{1,0:T(8,128)(2,1)} %param.23) | copy-start | bytes 6291460
  7.2 44.4 %all-gather.10.cloned.1.call-start = ((), (), s32[]{:S(2)}) async-start(), calls=%async_computation.6 | async-start | bytes 1572864 | tf_op jit(solution)/shard_map/all_gather | solution.py:55
  7.9 52.7 %all-gather.8.cloned.1.call-start = ((), (), s32[]{:S(2)}) async-start(), calls=%async_computation.5 | async-start | bytes 1572864 | tf_op jit(solution)/shard_map/all_gather | solution.py:54
  8.7 74.8 %all-gather.6.cloned.1.call-start = ((), (), s32[]{:S(2)}) async-start(), calls=%async_computation.4 | async-start | bytes 1572864 | tf_op jit(solution)/shard_map/all_gather | solution.py:56
  9.4 12.1 %copy-start.19 = (s32[32]{0:T(128)S(1)}, s32[32]{0:T(128)}, u32[]{:S(2)}) copy-start(s32[32]{0:T(128)} %param.15) | copy-start | bytes 388
  9.4 12.2 %copy-start.20 = (s32[32]{0:T(128)S(1)}, s32[32]{0:T(128)}, u32[]{:S(2)}) copy-start(s32[32]{0:T(128)} %param.18) | copy-start | bytes 388
  12.6 21.6 %all-to-all-start = ((bf16[320,16,32]{0,2,1:T(8,128)(2,1)}), bf16[320,16,32]{0,2,1:T(8,128)(2,1)S(1)}, u32[]{:S(2)}, u32[]{:S(2)}) async-start(bf16[320,16,32]{0,2,1:T(8,128)(2,1)} %all_to_all.38), calls=%async_computation | async-start | bytes 786432 | tf_op jit(solution)/shard_map/all_to_all | solution.py:47
  20.9 85.3 %all-gather.12.cloned.1.call-start = ((), (), s32[]{:S(2)}) async-start(), calls=%async_computation.7 | async-start | bytes 1572864 | tf_op jit(solution)/shard_map/all_gather | solution.py:112
  21.5 107.8 %all-reduce.3.cloned.1.call-start = ((), (), s32[]{:S(2)}) async-start(), calls=%async_computation.8 | async-start | bytes 786432 | tf_op jit(solution)/shard_map/psum | solution.py:114
  40.1 3.6 %copy-start.1 = (f32[16,5,64,32]{2,1,3,0:T(8,128)S(1)}, f32[16,5,64,32]{2,1,3,0:T(8,128)}, u32[]{:S(2)}) copy-start(f32[16,5,64,32]{2,1,3,0:T(8,128)} %reshape.233) | copy-start | bytes 1966084
  55.0 5.7 %copy-start.10 = (bf16[192,1024]{1,0:T(8,128)(2,1)S(1)}, bf16[192,1024]{1,0:T(8,128)(2,1)}, u32[]{:S(2)}) copy-start(bf16[192,1024]{1,0:T(8,128)(2,1)} %reshape.216) | copy-start | bytes 1179652
  67.5 4.3 %copy-start.2 = (bf16[32,64,8,64]{3,2,1,0:T(8,128)(2,1)S(1)}, bf16[32,64,8,64]{3,2,1,0:T(8,128)(2,1)}, u32[]{:S(2)}) copy-start(bf16[32,64,8,64]{3,2,1,0:T(8,128)(2,1)} %reshape.219) | copy-start | bytes 6291460
  68.0 8.5 %copy-start.6 = (f32[32,8,6,5]{2,3,1,0:T(8,128)}, f32[32,8,6,5]{2,3,1,0:T(8,128)S(1)}, u32[]{:S(2)}) copy-start(f32[32,8,6,5]{2,3,1,0:T(8,128)S(1)} %get-tuple-element.27) | copy-start | bytes 92164
  71.8 4.0 %copy-start.7 = (f32[32,8,6,32]{3,2,1,0:T(8,128)}, f32[32,8,6,32]{3,2,1,0:T(8,128)S(1)}, u32[]{:S(2)}) copy-start(f32[32,8,6,32]{3,2,1,0:T(8,128)S(1)} %get-tuple-element.29) | copy-start | bytes 589828
  87.9 4.0 %copy-start.12 = (bf16[160,512]{1,0:T(8,128)(2,1)}, bf16[160,512]{1,0:T(8,128)(2,1)S(1)}, u32[]{:S(2)}) copy-start(bf16[160,512]{1,0:T(8,128)(2,1)S(1)} %slice.42) | copy-start | bytes 491524
  93.0 3.9 %copy-start.17 = (f32[32,8,6]{2,1,0:T(8,128)S(1)}, f32[32,8,6]{2,1,0:T(8,128)}, u32[]{:S(2)}) copy-start(f32[32,8,6]{2,1,0:T(8,128)} %copy-done.16) | copy-start | bytes 18436
  96.9 3.5 %copy-start.5 = (bf16[32,64,8,64]{3,2,1,0:T(8,128)(2,1)S(1)}, bf16[32,64,8,64]{3,2,1,0:T(8,128)(2,1)}, u32[]{:S(2)}) copy-start(bf16[32,64,8,64]{3,2,1,0:T(8,128)(2,1)} %reshape.221) | copy-start | bytes 6291460
  96.9 3.7 %copy-start.21 = (f32[32,6,8,64]{3,1,2,0:T(8,128)S(1)}, f32[32,6,8,64]{3,1,2,0:T(8,128)}, u32[]{:S(2)}) copy-start(f32[32,6,8,64]{3,1,2,0:T(8,128)} %convolution_bitcast_fusion) | copy-start | bytes 1179652
  110.7 57.8 %reduce-scatter.2.cloned.1.call-start = ((), (), s32[]{:S(2)}) async-start(), calls=%async_computation.9 | async-start | bytes 1966080 | tf_op jit(solution)/shard_map/reduce_scatter | solution.py:122
  144.9 50.4 %all-gather.14.cloned.1.call-start = ((), (), s32[]{:S(2)}) async-start(), calls=%async_computation.10 | async-start | bytes 1966080 | tf_op jit(solution)/shard_map/all_gather | solution.py:126
  170.9 36.5 %copy-start.13 = (bf16[160,512]{1,0:T(8,128)(2,1)S(1)}, bf16[160,512]{1,0:T(8,128)(2,1)}, u32[]{:S(2)}) copy-start(bf16[160,512]{1,0:T(8,128)(2,1)} %copy-done.12) | copy-start | bytes 491524
  170.9 55.0 %all-reduce.5.cloned.1.call-start = ((), (), s32[]{:S(2)}) async-start(), calls=%async_computation.11 | async-start | bytes 655360 | tf_op jit(solution)/shard_map/psum | solution.py:130
  198.1 9.4 %copy-start.11 = (bf16[160,512]{1,0:T(8,128)(2,1)S(1)}, bf16[160,512]{1,0:T(8,128)(2,1)}, u32[]{:S(2)}) copy-start(bf16[160,512]{1,0:T(8,128)(2,1)} %slice.41) | copy-start | bytes 491524
  212.0 16.3 %copy-start.18 = (f32[1024]{0:T(1024)S(1)}, f32[1024]{0:T(1024)}, u32[]{:S(2)}) copy-start(f32[1024]{0:T(1024)} %param.25) | copy-start | bytes 12292
  (7 other events, 14.2 us)
Sparse Core Ops, SparseCore 0:
  9.5 28.2 all-gather.9
  39.3 21.2 all-gather.7
  62.2 21.2 all-gather.5
  84.9 21.2 all-gather.11
  110.8 18.3 all-reduce.2
  145.0 23.4 reduce-scatter.1
  171.0 24.2 all-gather.13
  207.5 18.3 all-reduce.4
where the time goes:
time: 238 us; the launch traced here: 236 us
  waiting for transfers between devices  94 us (39%)
  local copies, waits for them, and re-layouts  56.7 us (24%)
  matrix products  29.4 us (12%)
  blocking collectives  17.6 us (7%)
  other arithmetic  15.2 us (6%)
  between operations  14.6 us (6%)
  starting transfers between devices  8.88 us (4%)
    all_gather x1, waiting for transfers between devices, shards(): lax.all_gather(hidden, 'fsdp', axis=0, tiled=True)  24.3 us
    reduce_scatter x1, waiting for transfers between devices, shards(): lax.psum_scatter(matmul(halves, w_up).astype(jnp.bfloat16), 'fsdp', scatt...  23.3 us
    psum x1, waiting for transfers between devices, shards(): lax.psum(attn_part.astype(jnp.bfloat16), 'mp').astype(jnp.float32)  18.5 us
    dot_general x6, matrix products, matmul(): return jnp.dot(left, right, preferred_element_type=jnp.float32)  15.5 us
    psum x1, waiting for transfers between devices, shards(): lax.psum(down_part.astype(jnp.bfloat16), 'mp').astype(jnp.float32)  11 us
    convert_element_type x5, local copies, waits for them, and re-layouts, shards(): hidden_state = inputs.astype(jnp.float32) + attn_out[:, :frames, :]  10.6 us
    all_to_all x1, blocking collectives, shards(): lax.all_to_all(h_norm, 'fsdp', split_axis=1, concat_axis=0, tiled=True)  9.13 us
    all_to_all x1, blocking collectives, shards(): lax.all_to_all(down_all.astype(jnp.bfloat16), 'fsdp', split_axis=0, conca...  8.51 us
  transfers between devices with their start and end apart: 9, of which 7 were waited for; matrix products, arithmetic and copies ran while one was open for 32% of the time, Pallas kernels for 0%

commit v1 on v0

--- a/solution.py
+++ b/solution.py
@@ -111,7 +111,7 @@
     attended = attended.astype(jnp.bfloat16).reshape(streams * (frames + 1), head_cols)
     attn_part = matmul(attended, lax.all_gather(w_out, "fsdp", axis=1, tiled=True))
     attn_out = (
-        lax.psum(attn_part.astype(jnp.bfloat16), "mp")
+        jnp.sum(lax.all_gather(attn_part.astype(jnp.bfloat16), "mp"), axis=0)
         .astype(jnp.float32)
         .reshape(streams, frames + 1, width)
     )

time: 238 us -> 221 us (0.929)
  waiting for transfers between devices: 94 us -> 76.6 us
    psum x1 -> x0, waiting for transfers between devices: 18.5 us -> none  [shards(): lax.psum(attn_part.astype(jnp.bfloat16), 'mp').astype(jnp.float32)]
    unnamed x46 -> x45, local copies, waits for them, and re-layouts: 6.48 us -> 6.39 us
  transfers between devices with their start and end apart: 9 -> 8, of which waited for: 7 -> 6; matrix products, arithmetic and copies ran while one was open for 32% -> 34% of each run, Pallas kernels for 0% -> 0%
where the time goes in v1:
time: 221 us; the launch traced here: 220 us
  waiting for transfers between devices  76.6 us (35%)
  local copies, waits for them, and re-layouts  55 us (25%)
  matrix products  28.6 us (13%)
  blocking collectives  19.7 us (9%)
  other arithmetic  16.5 us (7%)
  between operations  14.6 us (7%)
  starting transfers between devices  8.62 us (4%)
    all_gather x1, waiting for transfers between devices, shards(): lax.all_gather(hidden, 'fsdp', axis=0, tiled=True)  24.3 us
    reduce_scatter x1, waiting for transfers between devices, shards(): lax.psum_scatter(matmul(halves, w_up).astype(jnp.bfloat16), 'fsdp', scatt...  23.4 us
    dot_general x6, matrix products, matmul(): return jnp.dot(left, right, preferred_element_type=jnp.float32)  14.7 us
    psum x1, waiting for transfers between devices, shards(): lax.psum(down_part.astype(jnp.bfloat16), 'mp').astype(jnp.float32)  12.1 us
    convert_element_type x5, local copies, waits for them, and re-layouts, shards(): hidden_state = inputs.astype(jnp.float32) + attn_out[:, :frames, :]  10.7 us
    all_to_all x1, blocking collectives, shards(): lax.all_to_all(h_norm, 'fsdp', split_axis=1, concat_axis=0, tiled=True)  8.84 us
    all_to_all x1, blocking collectives, shards(): lax.all_to_all(down_all.astype(jnp.bfloat16), 'fsdp', split_axis=0, conca...  8.51 us
    all_to_all x1, starting transfers between devices, shards(): lax.all_to_all(flattened, ('dp', 'fsdp'), split_axis=1, concat_axis=0, ti...  8.34 us
  transfers between devices with their start and end apart: 8, of which 6 were waited for; matrix products, arithmetic and copies ran while one was open for 34% of the time, Pallas kernels for 0%

profile of v1, /device:TPU:0, one launch (start us, length us, event | category | flops | bytes accessed | tf_op | source)
XLA Modules:
  0.0 219.7 jit_solution(16970803745782834515)
XLA Ops:
  12.5 8.3 %all-to-all-start = ((bf16[320,16,32]{0,2,1:T(8,128)(2,1)}), bf16[320,16,32]{0,2,1:T(8,128)(2,1)S(1)}, u32[]{:S(2)}, u32[]{:S(2)}) async-start(bf16[320,16,32]{0,2,1:T(8,128)(2,1)} %all_to_all.38), calls=%async_computation | async-start | bytes 786432 | tf_op jit(solution)/shard_map/all_to_all | solution.py:47
  21.6 6.2 %reshape.217 = bf16[32,64,8,64]{3,2,1,0:T(8,128)(2,1)} reshape(bf16[32,64,512]{2,1,0:T(8,128)(2,1)} %param.16) | data formatting | bytes 4194304 | tf_op jit(solution)/shard_map/reshape | solution.py:66
  27.8 6.2 %reshape.219 = bf16[32,64,8,64]{3,2,1,0:T(8,128)(2,1)} reshape(bf16[32,64,512]{2,1,0:T(8,128)(2,1)} %param.17) | data formatting | bytes 4194304 | tf_op jit(solution)/shard_map/reshape | solution.py:67
  40.1 3.6 %copy.120 = f32[32,5,16,64]{3,2,0,1:T(8,128)} copy(f32[32,5,16,64]{3,1,0,2:T(8,128)} %bitcast.54) | data formatting | bytes 1310720 | tf_op jit(solution)/shard_map/convert_element_type | solution.py:119
  51.6 3.4 %convolution_convert_fusion = bf16[1184,512]{1,0:T(8,128)(2,1)S(1)} fusion(bf16[1024,512]{1,0:T(8,128)(2,1)} %all-gather.11.cloned.1.call-done, bf16[1024,1024]{1,0:T(8,128)(2,1)} %bitcast.63, bf16[160,1024]{1,0:T(8,128)(2,1)} %multiply_convert_fusion.3), kind=kOutput, calls=%fused_computation.4 | convolution fusion | flops 1246969856 | bytes 4685824 | tf_op jit(solution)/shard_map/dot_general | solution.py:21
  56.7 3.9 %all-gather.9.cloned.1.call-done = bf16[1024,512]{1,0:T(8,128)(2,1)} async-done(((bf16[512,512]{1,0:T(8,128)(2,1)}), bf16[1024,512]{1,0:T(8,128)(2,1)}) %all-gather.9.cloned.1.call-update) | async-done | bytes 1048592 | tf_op jit(solution)/shard_map/all_gather | solution.py:54
  63.6 3.9 %reshape.216 = bf16[32,32,8,64]{3,2,1,0:T(8,128)(2,1)} reshape(bf16[1024,512]{1,0:T(8,128)(2,1)} %slice.40) | data formatting | bytes 2097152 | tf_op jit(solution)/shard_map/reshape | solution.py:64
  68.1 3.8 %fusion.62 = (f32[32,8,6]{2,1,0:T(8,128)S(1)}, f32[32,8,6,32]{3,2,1,0:T(8,128)S(1)}) fusion(bf16[32,32,8,64]{3,2,1,0:T(8,128)(2,1)} %reshape.216, bf16[32,6,8,64]{3,2,1,0:T(8,128)(2,1)S(1)} %reshape.215, pred[32,6,32]{2,1,0:T(8,128)(4,1)S(1)} %broadcast_and_fusion), kind=kOutput, calls=%fused_computation.93 | convolution fusion | flops 6437376 | bytes 1454080 | tf_op jit(solution)/shard_map/sqhd,skhd->shqk/dot_general | solution.py:77
  71.8 2.4 %fusion.63 = (f32[32,8,6]{2,1,0:T(8,128)S(1)}, f32[32,8,6,64]{3,2,1,0:T(8,128)S(1)}) fusion(bf16[32,64,8,64]{3,2,1,0:T(8,128)(2,1)S(1)} %copy-done.2, bf16[32,6,8,64]{3,2,1,0:T(8,128)(2,1)S(1)} %reshape.215, pred[32,64]{1,0:T(8,128)(4,1)S(1)} %iota_compare_fusion), kind=kOutput, calls=%fused_computation.94 | convolution fusion | flops 12876288 | bytes 2695168 | tf_op jit(solution)/shard_map/sqhd,skhd->shqk/dot_general | solution.py:80
  77.0 6.5 %all-gather.7.cloned.1.call-done = bf16[1024,512]{1,0:T(8,128)(2,1)} async-done(((bf16[512,512]{1,0:T(8,128)(2,1)}), bf16[1024,512]{1,0:T(8,128)(2,1)}) %all-gather.7.cloned.1.call-update) | async-done | bytes 1048592 | tf_op jit(solution)/shard_map/all_gather | solution.py:56
  83.5 3.4 %convolution_convert_fusion.1 = bf16[1184,512]{1,0:T(8,128)(2,1)S(1)} fusion(bf16[1024,512]{1,0:T(8,128)(2,1)} %all-gather.7.cloned.1.call-done, bf16[1024,1024]{1,0:T(8,128)(2,1)} %bitcast.64, bf16[160,1024]{1,0:T(8,128)(2,1)} %multiply_convert_fusion.3), kind=kOutput, calls=%fused_computation.5 | convolution fusion | flops 1246969856 | bytes 4685824 | tf_op jit(solution)/shard_map/dot_general | solution.py:21
  88.9 3.0 %convolution_bitcast_fusion = f32[32,6,8,64]{3,1,2,0:T(8,128)} fusion(f32[32,8,6,5]{2,3,1,0:T(8,128)} %copy-done.6, bf16[32,5,8,64]{3,2,1,0:T(8,128)(2,1)} %reshape.220, f32[32,8,6]{2,1,0:T(8,128)S(1)} %add_add_fusion, f32[32,8,6]{2,1,0:T(8,128)S(1)} %maximum_maximum_fusion), kind=kOutput, calls=%fused_computation.23 | convolution fusion | flops 1006080 | bytes 600064 | tf_op jit(solution)/shard_map/shqk,skhd->sqhd/dot_general | solution.py:108
  93.0 3.9 %reshape.213 = bf16[32,32,8,64]{3,2,1,0:T(8,128)(2,1)} reshape(bf16[1024,512]{1,0:T(8,128)(2,1)} %slice.38) | data formatting | bytes 2097152 | tf_op jit(solution)/shard_map/reshape | solution.py:65
  97.0 2.7 %fusion.8 = f32[32,6,8,64]{3,1,2,0:T(8,128)S(1)} fusion(bf16[32,32,8,64]{3,2,1,0:T(8,128)(2,1)} %reshape.213, f32[32,8,6,32]{3,2,1,0:T(8,128)} %copy-done.7, f32[32,8,6]{2,1,0:T(8,128)S(1)} %copy-done.16, f32[32,8,6]{2,1,0:T(8,128)S(1)} %maximum_maximum_fusion), kind=kOutput, calls=%fused_computation.17 | convolution fusion | flops 6438912 | bytes 1650688 | tf_op jit(solution)/shard_map/shqk,skhd->sqhd/dot_general | solution.py:104
  102.5 3.7 %all-gather.13.cloned.1.call-done = bf16[512,1024]{1,0:T(8,128)(2,1)} async-done(((bf16[512,512]{1,0:T(8,128)(2,1)}), bf16[512,1024]{1,0:T(8,128)(2,1)}) %all-gather.13.cloned.1.call-update) | async-done | bytes 1048592 | tf_op jit(solution)/shard_map/all_gather | solution.py:112
  107.8 2.4 %all-gather = bf16[384,1024]{1,0:T(8,128)(2,1)S(1)} all-gather(bf16[192,1024]{1,0:T(8,128)(2,1)S(1)} %convolution_convert_fusion.3), channel_id=2, replica_groups=mesh['dp'=8,'mp'=2,'fsdp'=2] {'mp'}, dimensions={0}, use_global_device_ids=true | all-gather | bytes 1179648 | tf_op jit(solution)/shard_map/all_gather | solution.py:114
  111.2 2.1 reshape.228
  117.5 8.8 %all_to_all.51 = bf16[160,2,512]{2,0,1:T(8,128)(2,1)S(1)} all-to-all(bf16[160,2,512]{2,0,1:T(8,128)(2,1)S(1)} %copy.142), channel_id=1, replica_groups=mesh['dp'=8,'mp'=2,'fsdp'=2] {'fsdp'}, dimensions={1} | all-to-all | bytes 655360 | tf_op jit(solution)/shard_map/all_to_all | solution.py:121
  128.4 23.4 %reduce-scatter.2.cloned.1.call-done = bf16[160,2048]{1,0:T(8,128)(2,1)} async-done(((bf16[320,2048]{1,0:T(8,128)(2,1)}), bf16[160,2048]{1,0:T(8,128)(2,1)}) %reduce-scatter.2.cloned.1.call-update) | async-done | bytes 655376 | tf_op jit(solution)/shard_map/reduce_scatter | solution.py:122
  151.8 2.4 %fusion.37 = bf16[160,2048]{1,0:T(8,128)(2,1)} fusion(bf16[160,2048]{1,0:T(8,128)(2,1)} %reduce-scatter.2.cloned.1.call-done), kind=kLoop, calls=%fused_computation.32 | loop fusion | flops 3276800 | bytes 1310720 | tf_op jit(solution)/shard_map/convert_element_type | solution.py:125
  154.2 24.3 %all-gather.15.cloned.1.call-done = bf16[320,2048]{1,0:T(8,128)(2,1)} async-done(((bf16[160,2048]{1,0:T(8,128)(2,1)}), bf16[320,2048]{1,0:T(8,128)(2,1)}) %all-gather.15.cloned.1.call-update) | async-done | bytes 1310736 | tf_op jit(solution)/shard_map/all_gather | solution.py:126
  178.6 2.8 %convolution_convert_fusion.4 = bf16[320,512]{1,0:T(8,128)(2,1)S(1)} fusion(bf16[320,2048]{1,0:T(8,128)(2,1)} %all-gather.15.cloned.1.call-done, bf16[2048,512]{1,0:T(8,128)(2,1)} %param.24), kind=kOutput, calls=%fused_computation.35 | convolution fusion | flops 671252480 | bytes 3735552 | tf_op jit(solution)/shard_map/dot_general | solution.py:21
  181.4 8.5 %all_to_all.52 = bf16[2,160,512]{2,1,0:T(8,128)(2,1)S(1)} all-to-all(bf16[2,160,512]{2,1,0:T(8,128)(2,1)S(1)} %bitcast.61), channel_id=1, replica_groups=mesh['dp'=8,'mp'=2,'fsdp'=2] {'fsdp'}, dimensions={0} | all-to-all | bytes 655360 | tf_op jit(solution)/shard_map/all_to_all | solution.py:127
  197.1 12.1 %all-reduce.2.cloned.1.call-done = bf16[160,1024]{1,0:T(8,128)(2,1)} async-done(((bf16[160,1024]{1,0:T(8,128)(2,1)}), bf16[160,1024]{1,0:T(8,128)(2,1)}) %all-reduce.2.cloned.1.call-update) | async-done | bytes 327696 | tf_op jit(solution)/shard_map/psum | solution.py:130
  (132 shorter events, 53.4 us)
Async XLA Ops:
  7.2 119.2 %copy-start = (bf16[512,2048]{1,0:T(8,128)(2,1)S(1)}, bf16[512,2048]{1,0:T(8,128)(2,1)}, u32[]{:S(2)}) copy-start(bf16[512,2048]{1,0:T(8,128)(2,1)} %param.23) | copy-start | bytes 6291460
  7.2 44.4 %all-gather.11.cloned.1.call-start = ((), (), s32[]{:S(2)}) async-start(), calls=%async_computation.6 | async-start | bytes 1572864 | tf_op jit(solution)/shard_map/all_gather | solution.py:55
  7.9 52.7 %all-gather.9.cloned.1.call-start = ((), (), s32[]{:S(2)}) async-start(), calls=%async_computation.5 | async-start | bytes 1572864 | tf_op jit(solution)/shard_map/all_gather | solution.py:54
  8.7 74.8 %all-gather.7.cloned.1.call-start = ((), (), s32[]{:S(2)}) async-start(), calls=%async_computation.4 | async-start | bytes 1572864 | tf_op jit(solution)/shard_map/all_gather | solution.py:56
  9.4 12.1 %copy-start.18 = (s32[32]{0:T(128)S(1)}, s32[32]{0:T(128)}, u32[]{:S(2)}) copy-start(s32[32]{0:T(128)} %param.15) | copy-start | bytes 388
  9.4 12.2 %copy-start.19 = (s32[32]{0:T(128)S(1)}, s32[32]{0:T(128)}, u32[]{:S(2)}) copy-start(s32[32]{0:T(128)} %param.18) | copy-start | bytes 388
  12.5 21.6 %all-to-all-start = ((bf16[320,16,32]{0,2,1:T(8,128)(2,1)}), bf16[320,16,32]{0,2,1:T(8,128)(2,1)S(1)}, u32[]{:S(2)}, u32[]{:S(2)}) async-start(bf16[320,16,32]{0,2,1:T(8,128)(2,1)} %all_to_all.38), calls=%async_computation | async-start | bytes 786432 | tf_op jit(solution)/shard_map/all_to_all | solution.py:47
  20.9 85.3 %all-gather.13.cloned.1.call-start = ((), (), s32[]{:S(2)}) async-start(), calls=%async_computation.7 | async-start | bytes 1572864 | tf_op jit(solution)/shard_map/all_gather | solution.py:112
  21.5 130.3 %reduce-scatter.2.cloned.1.call-start = ((), (), s32[]{:S(2)}) async-start(), calls=%async_computation.8 | async-start | bytes 1966080 | tf_op jit(solution)/shard_map/reduce_scatter | solution.py:122
  40.1 3.6 %copy-start.1 = (f32[16,5,64,32]{2,1,3,0:T(8,128)S(1)}, f32[16,5,64,32]{2,1,3,0:T(8,128)}, u32[]{:S(2)}) copy-start(f32[16,5,64,32]{2,1,3,0:T(8,128)} %reshape.230) | copy-start | bytes 1966084
  55.0 5.7 %copy-start.9 = (bf16[192,1024]{1,0:T(8,128)(2,1)S(1)}, bf16[192,1024]{1,0:T(8,128)(2,1)}, u32[]{:S(2)}) copy-start(bf16[192,1024]{1,0:T(8,128)(2,1)} %reshape.214) | copy-start | bytes 1179652
  67.5 4.3 %copy-start.2 = (bf16[32,64,8,64]{3,2,1,0:T(8,128)(2,1)S(1)}, bf16[32,64,8,64]{3,2,1,0:T(8,128)(2,1)}, u32[]{:S(2)}) copy-start(bf16[32,64,8,64]{3,2,1,0:T(8,128)(2,1)} %reshape.217) | copy-start | bytes 6291460
  68.1 8.5 %copy-start.6 = (f32[32,8,6,5]{2,3,1,0:T(8,128)}, f32[32,8,6,5]{2,3,1,0:T(8,128)S(1)}, u32[]{:S(2)}) copy-start(f32[32,8,6,5]{2,3,1,0:T(8,128)S(1)} %get-tuple-element.27) | copy-start | bytes 92164
  71.8 4.0 %copy-start.7 = (f32[32,8,6,32]{3,2,1,0:T(8,128)}, f32[32,8,6,32]{3,2,1,0:T(8,128)S(1)}, u32[]{:S(2)}) copy-start(f32[32,8,6,32]{3,2,1,0:T(8,128)S(1)} %get-tuple-element.29) | copy-start | bytes 589828
  87.9 4.0 %copy-start.11 = (bf16[160,512]{1,0:T(8,128)(2,1)}, bf16[160,512]{1,0:T(8,128)(2,1)S(1)}, u32[]{:S(2)}) copy-start(bf16[160,512]{1,0:T(8,128)(2,1)S(1)} %slice.42) | copy-start | bytes 491524
  88.9 3.1 %copy-start.15 = (f32[32,8,6]{2,1,0:T(8,128)}, f32[32,8,6]{2,1,0:T(8,128)S(1)}, u32[]{:S(2)}) copy-start(f32[32,8,6]{2,1,0:T(8,128)S(1)} %add_add_fusion) | copy-start | bytes 18436
  93.0 3.9 %copy-start.16 = (f32[32,8,6]{2,1,0:T(8,128)S(1)}, f32[32,8,6]{2,1,0:T(8,128)}, u32[]{:S(2)}) copy-start(f32[32,8,6]{2,1,0:T(8,128)} %copy-done.15) | copy-start | bytes 18436
  97.0 3.5 %copy-start.5 = (bf16[32,64,8,64]{3,2,1,0:T(8,128)(2,1)S(1)}, bf16[32,64,8,64]{3,2,1,0:T(8,128)(2,1)}, u32[]{:S(2)}) copy-start(bf16[32,64,8,64]{3,2,1,0:T(8,128)(2,1)} %reshape.219) | copy-start | bytes 6291460
  97.0 3.7 %copy-start.20 = (f32[32,6,8,64]{3,1,2,0:T(8,128)S(1)}, f32[32,6,8,64]{3,1,2,0:T(8,128)}, u32[]{:S(2)}) copy-start(f32[32,6,8,64]{3,1,2,0:T(8,128)} %convolution_bitcast_fusion) | copy-start | bytes 1179652
  128.4 50.2 %all-gather.15.cloned.1.call-start = ((), (), s32[]{:S(2)}) async-start(), calls=%async_computation.9 | async-start | bytes 1966080 | tf_op jit(solution)/shard_map/all_gather | solution.py:126
  154.2 55.0 %all-reduce.2.cloned.1.call-start = ((), (), s32[]{:S(2)}) async-start(), calls=%async_computation.10 | async-start | bytes 655360 | tf_op jit(solution)/shard_map/psum | solution.py:130
  181.4 10.7 %copy-start.12 = (bf16[160,512]{1,0:T(8,128)(2,1)S(1)}, bf16[160,512]{1,0:T(8,128)(2,1)}, u32[]{:S(2)}) copy-start(bf16[160,512]{1,0:T(8,128)(2,1)} %copy-done.11) | copy-start | bytes 491524
  181.4 10.8 %copy-start.10 = (bf16[160,512]{1,0:T(8,128)(2,1)S(1)}, bf16[160,512]{1,0:T(8,128)(2,1)}, u32[]{:S(2)}) copy-start(bf16[160,512]{1,0:T(8,128)(2,1)} %slice.41) | copy-start | bytes 491524
  192.3 19.3 %copy-start.17 = (f32[1024]{0:T(1024)S(1)}, f32[1024]{0:T(1024)}, u32[]{:S(2)}) copy-start(f32[1024]{0:T(1024)} %param.25) | copy-start | bytes 12292
  (5 other events, 10.2 us)
Sparse Core Ops, SparseCore 0:
  9.5 28.2 all-gather.10
  39.3 21.2 all-gather.8
  62.2 21.2 all-gather.6
  84.9 21.2 all-gather.12
  128.5 23.2 reduce-scatter.1
  154.3 24.2 all-gather.14
  190.8 18.3 all-reduce.1
